TPU v7x, 32 devices: a whole 2x2x4 slice. The times are simulated.
32 devices in a mesh: owner: 4 (over x, core), rows: 8 (over z, y).
Axes of the slice: x: 2, y: 2, z: 4, core: 2. Of those that a mesh axis runs over, the one named last changes fastest.
Arguments:
- train_gate: float32 [128, 2048, 768], P('owner', 'rows'), may hold values from -0.1875 to 0.1875
- train_up: float32 [128, 2048, 768], P('owner', 'rows'), may hold values from -0.1875 to 0.1875
- router_weight: float32 [2048, 128], P('rows', 'owner'), may hold values from -0.125 to 0.125
- router_gain: float32 [2048], P('rows'), may hold values from 0.25 to 1.75
Outputs:
- ready_gate: bfloat16 [128, 2048, 768], P(('owner', 'rows'))
- ready_up: bfloat16 [128, 2048, 768], P(('owner', 'rows'))
- scale_gate: float32 [128, 768], P(('owner', 'rows'))
- scale_up: float32 [128, 768], P(('owner', 'rows'))
- serve_router: bfloat16 [2048, 128], replicated
All inputs are finite; a program needn't handle non-finite values.
Results may differ from a plain program's by a relative error of at most 0.001.
Values may be sent and summed in bfloat16 or wider, within the bound.
A program may use at most 192 MiB of HBM per device.

v0:
```python
import jax
import jax.numpy as jnp
from jax import lax
from jax.sharding import PartitionSpec as P


def on_device(train_gate, train_up, router_weight, router_gain):
    total_gate, total_up = lax.psum(
        (jnp.sum(train_gate * train_gate, axis=1), jnp.sum(train_up * train_up, axis=1)), "rows"
    )
    scale_gate = jnp.sqrt(total_gate)
    scale_up = jnp.sqrt(total_up)
    narrow_gate, narrow_up = (
        (train_gate / jnp.expand_dims(scale_gate, 1)).astype(jnp.bfloat16),
        (train_up / jnp.expand_dims(scale_up, 1)).astype(jnp.bfloat16),
    )
    ready_gate, ready_up = (
        lax.all_to_all(narrow_gate, "rows", split_axis=0, concat_axis=1, tiled=True),
        lax.all_to_all(narrow_up, "rows", split_axis=0, concat_axis=1, tiled=True),
    )
    scale_gate = lax.dynamic_slice_in_dim(
        scale_gate, lax.axis_index("rows") * ready_gate.shape[0], ready_gate.shape[0], axis=0
    )
    scale_up = lax.dynamic_slice_in_dim(
        scale_up, lax.axis_index("rows") * ready_up.shape[0], ready_up.shape[0], axis=0
    )
    part_router = (router_weight * router_gain[:, None]).astype(jnp.bfloat16)
    row_router = lax.all_gather(part_router, "rows", axis=0, tiled=True)
    serve_router = lax.all_gather(row_router, "owner", axis=1, tiled=True)
    return (ready_gate, ready_up, scale_gate, scale_up, serve_router)


def solution(mesh):
    return jax.shard_map(
        on_device,
        mesh=mesh,
        in_specs=(
            P("owner", "rows", None),
            P("owner", "rows", None),
            P("rows", "owner"),
            P("rows"),
        ),
        out_specs=(
            P(("owner", "rows"), None, None),
            P(("owner", "rows"), None, None),
            P(("owner", "rows"), None),
            P(("owner", "rows"), None),
            P(),
        ),
        check_vma=False,
    )
```

profile of v0, /device:TPU:0, one launch (start us, length us, event | category | flops | bytes accessed | tf_op | source)
XLA Modules:
  0.0 723.9 jit_solution(15116092223100259474)
XLA Ops:
  7.2 0.0 all-reduce.3.cloned.1.call-start
  7.2 17.3 %multiply_reduce_fusion = (f32[32,768]{1,0:T(8,128)}, f32[32,768]{1,0:T(8,128)}) fusion(f32[32,256,768]{2,1,0:T(8,128)} %param.5, f32[32,256,768]{2,1,0:T(8,128)} %param.4), kind=kLoop, calls=%fused_computation.1 | loop fusion | flops 25116672 | bytes 50528256 | tf_op jit(solution)/shard_map/reduce_sum | solution.py:9
  24.5 0.0 all-reduce.3.cloned.1.call-update
  24.5 73.8 %all-reduce.3.cloned.1.call-done = (f32[32,768]{1,0:T(8,128)}, f32[32,768]{1,0:T(8,128)}) async-done(((f32[32,768]{1,0:T(8,128)}, f32[32,768]{1,0:T(8,128)}), (f32[32,768]{1,0:T(8,128)}, f32[32,768]{1,0:T(8,128)})) %all-reduce.3.cloned.1.call-update) | async-done | bytes 196624 | tf_op jit(solution)/shard_map/psum | solution.py:8
  98.2 0.9 sqrt.6
  99.2 0.0 copy-start
  99.2 13.7 %divide_convert_fusion.1 = bf16[32,256,768]{2,1,0:T(8,128)(2,1)} fusion(f32[32,256,768]{2,1,0:T(8,128)} %param.4, f32[32,768]{1,0:T(8,128)S(1)} %sqrt.6), kind=kLoop, calls=%fused_computation.2 | loop fusion | flops 12582912 | bytes 37847040 | tf_op jit(solution)/shard_map/convert_element_type | solution.py:14
  112.9 5.4 all-to-all-start
  118.2 0.0 copy-done
  118.3 0.0 copy-start.1
  118.3 0.0 copy-start.2
  118.3 13.8 %divide_convert_fusion = bf16[32,256,768]{2,1,0:T(8,128)(2,1)} fusion(f32[32,256,768]{2,1,0:T(8,128)} %param.5, f32[32,768]{1,0:T(8,128)S(1)} %sqrt.7), kind=kLoop, calls=%fused_computation | loop fusion | flops 12582912 | bytes 37847040 | tf_op jit(solution)/shard_map/convert_element_type | solution.py:15
  132.1 257.3 %all-to-all-done = bf16[32,256,768]{2,1,0:T(8,128)(2,1)} async-done(((bf16[32,256,768]{2,1,0:T(8,128)(2,1)}), bf16[32,256,768]{2,1,0:T(8,128)(2,1)}, u32[]{:S(2)}, u32[]{:S(2)}) %all-to-all-start) | async-done | bytes 12582944 | tf_op jit(solution)/shard_map/all_to_all | solution.py:18
  389.4 5.4 all-to-all-start.1
  394.8 0.0 copy-done.1
  394.8 0.0 copy-done.2
  394.8 291.6 %all_gather.6 = bf16[2048,32]{0,1:T(8,128)(2,1)S(1)} all-gather(bf16[256,32]{0,1:T(8,128)(2,1)S(1)} %multiply_convert_fusion), channel_id=1, replica_groups=mesh['owner'=4,'rows'=8] {'rows'}, dimensions={0}, use_global_device_ids=true | all-gather | bytes 147456 | tf_op jit(solution)/shard_map/all_gather | solution.py:28
  686.4 7.1 all_gather.7
  693.5 1.0 copy.14
  694.5 0.6 constant_dynamic-slice_fusion
  695.1 0.6 constant_dynamic-slice_fusion.1
  695.7 10.7 %copy.12 = bf16[8,4,256,768]{3,2,0,1:T(8,128)(2,1)} copy(bf16[8,4,256,768]{3,2,1,0:T(8,128)(2,1)} %bitcast) | data formatting | bytes 25165824 | tf_op jit(solution)/shard_map/all_to_all | solution.py:18
  706.4 0.0 all-to-all-done.1
  706.4 10.7 %copy.13 = bf16[8,4,256,768]{3,2,0,1:T(8,128)(2,1)} copy(bf16[8,4,256,768]{3,2,1,0:T(8,128)(2,1)} %bitcast.3) | data formatting | bytes 25165824 | tf_op jit(solution)/shard_map/all_to_all | solution.py:19
  (2 shorter events, 0.0 us)
Async XLA Ops:
  7.2 91.1 %all-reduce.3.cloned.1.call-start = ((), (), s32[]{:S(2)}) async-start(), calls=%async_computation.2 | async-start | bytes 393216 | tf_op jit(solution)/shard_map/psum | solution.py:8
  99.2 19.1 %copy-start = (f32[32,768]{1,0:T(8,128)S(1)}, f32[32,768]{1,0:T(8,128)}, u32[]{:S(2)}) copy-start(f32[32,768]{1,0:T(8,128)} %get-tuple-element.11) | copy-start | bytes 294916
  112.9 276.5 %all-to-all-start = ((bf16[32,256,768]{2,1,0:T(8,128)(2,1)}), bf16[32,256,768]{2,1,0:T(8,128)(2,1)}, u32[]{:S(2)}, u32[]{:S(2)}) async-start(bf16[32,256,768]{2,1,0:T(8,128)(2,1)} %divide_convert_fusion.1), calls=%async_computation | async-start | bytes 25165824 | tf_op jit(solution)/shard_map/all_to_all | solution.py:18
  118.3 276.5 %copy-start.1 = (f32[256,32]{0,1:T(8,128)S(1)}, f32[256,32]{0,1:T(8,128)}, u32[]{:S(2)}) copy-start(f32[256,32]{0,1:T(8,128)} %param.6) | copy-start | bytes 98308
  118.3 276.5 %copy-start.2 = (f32[256]{0:T(256)S(1)}, f32[256]{0:T(256)}, u32[]{:S(2)}) copy-start(f32[256]{0:T(256)} %param.7) | copy-start | bytes 3076
  389.4 317.0 %all-to-all-start.1 = ((bf16[32,256,768]{2,1,0:T(8,128)(2,1)}), bf16[32,256,768]{2,1,0:T(8,128)(2,1)}, u32[]{:S(2)}, u32[]{:S(2)}) async-start(bf16[32,256,768]{2,1,0:T(8,128)(2,1)} %divide_convert_fusion), calls=%async_computation.1 | async-start | bytes 25165824 | tf_op jit(solution)/shard_map/all_to_all | solution.py:19
Sparse Core Ops, SparseCore 0:
  24.6 73.5 all-reduce.2
where the time goes:
time: 724 us
  waiting for transfers between devices  331 us (46%)
  blocking collectives  299 us (41%)
  other arithmetic  44.7 us (6%)
  local copies, waits for them, and re-layouts  24.5 us (3%)
  between operations  14.1 us (2%)
  starting transfers between devices  10.8 us (1%)
    all_gather x1, blocking collectives, on_device(): row_router = lax.all_gather(part_router, 'rows', axis=0, tiled=True)  292 us
    all_to_all x1, waiting for transfers between devices, on_device(): lax.all_to_all(narrow_gate, 'rows', split_axis=0, concat_axis=1, tiled=True)  257 us
    psum x1, waiting for transfers between devices, on_device(): lax.psum((jnp.sum(train_gate * train_gate, axis=1), jnp.sum(train_up * tr...  73.8 us
    reduce_sum x1, other arithmetic, on_device(): jnp.sum(train_up * train_up, axis=1)  17.3 us
  transfers between devices with their start and end apart: 3, of which 2 were waited for; matrix products, arithmetic and copies ran while one was open for 4% of the time, Pallas kernels for 0%

commit v1 on v0

v1 whole, which is shorter than its diff:
```python
import functools

import jax
import jax.numpy as jnp
from jax import lax
from jax.experimental import pallas as pl
from jax.experimental.pallas import tpu as pltpu
from jax.sharding import PartitionSpec as P

MESH = pl.DeviceIdType.MESH
CHUNK = 32


def pairing(n, me, k):
    if n & (n - 1):
        return lax.rem(me + k, n), lax.rem(me + n - k, n)
    other, bit = 0, 1
    while bit < n:
        own = (me // bit) % 2
        other = other + bit * ((1 - own) if k & bit else own)
        bit *= 2
    return other, other


def kernel(
    rows_n, owners_n,
    gate, up, weight, gain,
    ready_gate, ready_up, scale, router,
    slabs, send, part, gathered, scales, mine,
    load_sem, data_send, data_recv, sum_send, sum_recv, scale_send, scale_recv,
    own_sem, router_send, router_recv, router_own, forward_send, forward_recv,
):
    me, group = lax.axis_index("rows"), lax.axis_index("owner")
    height, width = gate.shape[2], gate.shape[3]
    each = gate.shape[1]
    steps = 2 * each
    far_first = list(range(rows_n - 1, -1, -1))
    place = [pairing(rows_n, me, k) for k in range(rows_n)]
    here = pl.ds(pl.multiple_of(me * height, height), height)

    def load(step, slab):
        bank, c = (gate, up)[step // each], step % each
        return [
            pltpu.make_async_copy(bank.at[place[k][0], c], slabs.at[slab, k], load_sem.at[slab, k])
            for k in range(rows_n)
        ]

    def begin(copies):
        for copy in copies:
            copy.start()

    def sum_one(slab, k, step):
        def add(i, total):
            x = slabs[slab, k, pl.ds(i * CHUNK, CHUNK), :]
            return total + jnp.sum((x * x).reshape(CHUNK // 8, 8, width), axis=0)

        total = lax.fori_loop(0, height // CHUNK, add, jnp.zeros((8, width), jnp.float32))
        part[place[k][0], step] = jnp.sum(total, axis=0, keepdims=True)

    def sum_copies(which, lo, hi):
        return [
            pltpu.make_async_remote_copy(
                part.at[place[k][0], pl.ds(lo, hi - lo)],
                gathered.at[me, pl.ds(lo, hi - lo)],
                sum_send.at[which, k], sum_recv.at[which, k],
                device_id={"rows": place[k][0]}, device_id_type=MESH,
            )
            for k in far_first[:-1]
        ]

    def scale_copies(which, lo, hi):
        return [
            pltpu.make_async_remote_copy(
                scales.at[me, pl.ds(lo, hi - lo)],
                scales.at[me, pl.ds(lo, hi - lo)],
                scale_send.at[which, k], scale_recv.at[which, k],
                device_id={"rows": place[k][0]}, device_id_type=MESH,
            )
            for k in far_first[:-1]
        ]

    def finish_sums(lo, hi):
        for step in range(lo, hi):
            gathered[me, step] = part[me, step]
        for step in range(lo, hi):
            total = gathered[0, step]
            for source in range(1, rows_n):
                total = total + gathered[source, step]
            root = jnp.sqrt(total)
            scales[me, step] = root
            scale[step] = root

    def data_copy(step, k):
        bank, c = (ready_gate, ready_up)[step // each], step % each
        if k == 0:
            return pltpu.make_async_copy(send.at[step, 0], bank.at[c, here], own_sem.at[step])
        return pltpu.make_async_remote_copy(
            send.at[step, k], bank.at[c, here], data_send.at[step, k], data_recv.at[step, k],
            device_id={"rows": place[k][0]}, device_id_type=MESH,
        )

    def ship(slab, k, step):
        by = scales[place[k][0], step]

        def narrow(i, carry):
            at = pl.ds(i * CHUNK, CHUNK)
            send[step, k, at, :] = (slabs[slab, k, at, :] / by).astype(jnp.bfloat16)
            return carry

        lax.fori_loop(0, height // CHUNK, narrow, 0)
        data_copy(step, k).start()

    first, second = load(0, 0), load(1, 1)
    begin([first[k] for k in far_first])
    begin([second[k] for k in far_first])

    barrier = pltpu.get_barrier_semaphore()
    for k in range(1, rows_n):
        pl.semaphore_signal(barrier, inc=1, device_id={"rows": place[k][0]}, device_id_type=MESH)
    for j in range(1, owners_n):
        pl.semaphore_signal(
            barrier, inc=1, device_id={"owner": lax.rem(group + j, owners_n)}, device_id_type=MESH
        )

    mine[...] = (weight[...] * gain[...]).astype(jnp.bfloat16)

    for k in far_first:
        first[k].wait()
        sum_one(0, k, 0)
    pl.semaphore_wait(barrier, rows_n + owners_n - 2)
    first_sums = sum_copies(0, 0, 1)
    begin(first_sums)
    for copy in first_sums:
        copy.wait_recv()
    finish_sums(0, 1)
    first_scales = scale_copies(0, 0, 1)
    begin(first_scales)
    for copy in first_scales:
        copy.wait_recv()

    lots = far_first[: rows_n // 4], far_first[rows_n // 4 : rows_n // 4 + rows_n // 8], far_first[rows_n // 4 + rows_n // 8 :]
    for k in lots[0]:
        ship(0, k, 0)

    columns = pl.ds(pl.multiple_of(me * height, height), height)
    router_copies = [
        pltpu.make_async_remote_copy(
            mine, router.at[group, :, columns], router_send.at[k], router_recv.at[k],
            device_id={"rows": place[k][0]}, device_id_type=MESH,
        )
        for k in far_first[:-1]
    ]
    router_local = pltpu.make_async_copy(mine, router.at[group, :, columns], router_own)
    router_local.start()

    waiting = second
    for step in range(1, steps):
        slab = 1 + (step - 1) % 2
        now = waiting
        if step + 1 < steps:
            waiting = load(step + 1, 1 + step % 2)
            begin(waiting)
        for k in range(rows_n):
            now[k].wait()
            sum_one(slab, k, step)
    rest_sums = sum_copies(1, 1, steps)
    begin(rest_sums)
    begin(router_copies)
    waiting = load(1, 1)
    begin(waiting)
    for k in lots[1]:
        ship(0, k, 0)
    for copy in rest_sums:
        copy.wait_recv()
    finish_sums(1, steps)
    rest_scales = scale_copies(1, 1, steps)
    begin(rest_scales)
    for k in lots[2]:
        ship(0, k, 0)
    for copy in rest_scales:
        copy.wait_recv()

    for step in range(1, steps):
        slab = 1 + (step - 1) % 2
        now = waiting
        if step + 1 < steps:
            waiting = load(step + 1, 1 + step % 2)
            begin(waiting)
        for k in far_first:
            now[k].wait()
            ship(slab, k, step)

    for copy in router_copies:
        copy.wait_recv()
    router_local.wait()
    forwards = []
    for j in range(1, owners_n):
        forwards.append(
            pltpu.make_async_remote_copy(
                router.at[group], router.at[group], forward_send.at[j], forward_recv.at[j],
                device_id={"owner": lax.rem(group + j, owners_n)}, device_id_type=MESH,
            )
        )
    begin(forwards)

    for copies in (first_sums, first_scales, rest_sums, rest_scales, router_copies):
        for copy in copies:
            copy.wait_send()
    for copy in forwards:
        copy.wait()
    for step in range(steps):
        for k in far_first:
            data_copy(step, k).wait()


def on_device(rows_n, owners_n, train_gate, train_up, router_weight, router_gain):
    experts, height, width = train_gate.shape
    each = experts // rows_n
    steps = 2 * each
    cols = router_weight.shape[1]
    f32, bf16, dma = jnp.float32, jnp.bfloat16, pltpu.SemaphoreType.DMA
    hbm, vmem = pl.BlockSpec(memory_space=pl.ANY), pl.BlockSpec(memory_space=pltpu.VMEM)
    ready = jax.ShapeDtypeStruct((each, rows_n * height, width), bf16)
    ready_gate, ready_up, scale, router = pl.pallas_call(
        functools.partial(kernel, rows_n, owners_n),
        out_shape=(
            ready,
            ready,
            jax.ShapeDtypeStruct((steps, 1, width), f32),
            jax.ShapeDtypeStruct((owners_n, cols, rows_n * height), bf16),
        ),
        in_specs=[hbm, hbm, vmem, vmem],
        out_specs=(hbm, hbm, vmem, hbm),
        scratch_shapes=[
            pltpu.VMEM((3, rows_n, height, width), f32),
            pltpu.VMEM((steps, rows_n, height, width), bf16),
            pltpu.VMEM((rows_n, steps, 1, width), f32),
            pltpu.VMEM((rows_n, steps, 1, width), f32),
            pltpu.VMEM((rows_n, steps, 1, width), f32),
            pltpu.VMEM((cols, height), bf16),
            dma((3, rows_n)),
            dma((steps, rows_n)),
            dma((steps, rows_n)),
            dma((2, rows_n)),
            dma((2, rows_n)),
            dma((2, rows_n)),
            dma((2, rows_n)),
            dma((steps,)),
            dma((rows_n,)),
            dma((rows_n,)),
            dma,
            dma((owners_n,)),
            dma((owners_n,)),
        ],
        compiler_params=pltpu.CompilerParams(
            collective_id=0, has_side_effects=True, vmem_limit_bytes=60 * 1024 * 1024
        ),
        name="serve",
    )(
        train_gate.reshape(rows_n, each, height, width),
        train_up.reshape(rows_n, each, height, width),
        router_weight.T,
        router_gain[None, :],
    )
    serve_router = router.reshape(owners_n * cols, rows_n * height).T
    scale = scale.reshape(steps, width)
    return (ready_gate, ready_up, scale[:each], scale[each:], serve_router)


def solution(mesh):
    return jax.shard_map(
        functools.partial(on_device, mesh.shape["rows"], mesh.shape["owner"]),
        mesh=mesh,
        in_specs=(
            P("owner", "rows", None),
            P("owner", "rows", None),
            P("rows", "owner"),
            P("rows"),
        ),
        out_specs=(
            P(("owner", "rows"), None, None),
            P(("owner", "rows"), None, None),
            P(("owner", "rows"), None),
            P(("owner", "rows"), None),
            P(),
        ),
        check_vma=False,
    )
```

time: 724 us -> 604 us (0.83)
  Pallas kernels: 0 us -> 579 us
  waiting for transfers between devices: 331 us -> 0 us
  blocking collectives: 299 us -> 0 us
  other arithmetic: 44.7 us -> 0 us
  between operations: 14.1 us -> 0.64 us
  starting transfers between devices: 10.8 us -> 0 us
    pallas_call x0 -> x1, Pallas kernels: none -> 579 us  [on_device(): pl.pallas_call(functools.partial(kernel, rows_n, owners_n), out_shape=(re...]
    all_gather x2 -> x0, blocking collectives: 299 us -> none  [the longest x1 292 us: on_device(): row_router = lax.all_gather(part_router, 'rows', axis=0, tiled=True)]
    all_to_all x2 -> x0, waiting for transfers between devices: 257 us -> none  [the longest x1 257 us: on_device(): lax.all_to_all(narrow_gate, 'rows', split_axis=0, concat_axis=1, tiled=True)]
    psum x1 -> x0, waiting for transfers between devices: 73.8 us -> none  [on_device(): lax.psum((jnp.sum(train_gate * train_gate, axis=1), jnp.sum(train_up * tr...]
    convert_element_type x3 -> x0, other arithmetic: 27.5 us -> none  [the longest x1 13.8 us: on_device(): (train_up / jnp.expand_dims(scale_up, 1)).astype(jnp.bfloat16)]
    all_to_all x2 -> x0, local copies, waits for them, and re-layouts: 21.4 us -> none  [the longest x1 10.7 us: on_device(): lax.all_to_all(narrow_up, 'rows', split_axis=0, concat_axis=1, tiled=True)]
    unnamed x7 -> x5, local copies, waits for them, and re-layouts: 1.02 us -> 18.4 us
    reduce_sum x1 -> x0, other arithmetic: 17.3 us -> none  [on_device(): jnp.sum(train_up * train_up, axis=1)]
  transfers between devices with their start and end apart: 3 -> 0, of which waited for: 2 -> 0; matrix products, arithmetic and copies ran while one was open for 4% -> 0% of each run, Pallas kernels for 0% -> 0%
where the time goes in v1:
time: 604 us; the launch traced here: 601 us
  Pallas kernels  579 us (96%)
  local copies, waits for them, and re-layouts  21.2 us (4%)
    pallas_call x1, Pallas kernels, on_device(): pl.pallas_call(functools.partial(kernel, rows_n, owners_n), out_shape=(re...  579 us
    unnamed x5, local copies, waits for them, and re-layouts  18.4 us

profile of v1, /device:TPU:0, one launch (start us, length us, event | category | flops | bytes accessed | tf_op | source)
XLA Modules:
  0.0 601.3 jit_solution(12116874426812339928)
XLA Ops:
  0.6 579.5 %serve.1 = (bf16[4,2048,768]{2,1,0:T(8,128)(2,1)}, bf16[4,2048,768]{2,1,0:T(8,128)(2,1)}, f32[8,1,768]{2,1,0:T(1,128)}, bf16[4,32,2048]{2,1,0:T(8,128)(2,1)}) custom-call(f32[8,4,256,768]{3,2,1,0:T(8,128)} %bitcast.10, f32[8,4,256,768]{3,2,1,0:T(8,128)} %bitcast.11, f32[32,256]{1,0:T(8,128)} %bitcast.14, f32[1,256]{1,0:T(1,128)} %bitcast.15), custom_call_target="tpu_custom_call" | custom-call | tf_op jit(solution)/shard_map/serve/pallas_call | solution.py:224
  580.1 0.7 fusion
  580.8 0.6 copy_bitcast_fusion
  581.4 2.0 copy.9
  583.5 0.0 copy-start
  583.5 11.0 %copy.16 = bf16[4,2048,768]{2,1,0:T(8,128)(2,1)} copy(bf16[4,2048,768]{2,1,0:T(8,128)(2,1)} %get-tuple-element.22) | data formatting | bytes 25165824
  594.5 2.0 copy-done
  596.5 4.8 copy.17
Async XLA Ops:
  583.5 13.0 %copy-start = (bf16[4,2048,768]{2,1,0:T(8,128)(2,1)S(1)}, bf16[4,2048,768]{2,1,0:T(8,128)(2,1)}, u32[]{:S(2)}) copy-start(bf16[4,2048,768]{2,1,0:T(8,128)(2,1)} %get-tuple-element.23) | copy-start | bytes 37748740
